TPU v7x, 256 devices: a whole 4x4x8 slice. The times are simulated.
256 devices in a mesh: tok: 8 (over x, core), col: 32 (over y, z).
Axes of the slice: x: 4, y: 4, z: 8, core: 2. Of those that a mesh axis runs over, the one named last changes fastest.
Arguments:
- hidden_in: bfloat16 [2048, 36864], P('tok', 'col'), may hold values from -6 to 6
- down_weight: bfloat16 [4608, 36864], P('col', 'tok'), may hold values from -0.046875 to 0.046875
- keep_mask: int32 [4608, 36864], P('col', 'tok'), may hold values 0 or 1
Outputs:
- layer_out: bfloat16 [2048, 4608], P(('tok', 'col'))
- hessian: float32 [4608, 4608], P('col', 'tok')
All inputs are finite; a program needn't handle non-finite values. No bound on the sum of `keep_mask` on one device may be relied on, other than what follows from the above.
Results may differ from a plain program's by a relative error of at most 0.012.
Values may be sent and summed in bfloat16 or wider, within the bound.
A program may use at most 128 MiB of HBM per device.

v0:
```python
import jax
import jax.numpy as jnp
from jax import lax
from jax.sharding import PartitionSpec as P


def laid_out(pieces, dim):
    lengths = list(pieces.shape[1:])
    lengths[dim] *= pieces.shape[0]
    return jnp.moveaxis(pieces, 0, dim).reshape(lengths)


def from_everyone(x, axis):
    size = lax.axis_size(axis)
    return lax.all_to_all(jnp.broadcast_to(x[None], (size, *x.shape)), axis, 0, 0, tiled=True)


def gathered_copies(x, axis, dim):
    return laid_out(from_everyone(x, axis), dim)


def split_up(x, dim, size):
    before, after = (x.shape[:dim], x.shape[dim + 1 :])
    return jnp.moveaxis(x.reshape(*before, size, -1, *after), dim, 0)


def sent_and_summed(x, axis, dim):
    pieces = split_up(x, dim, lax.axis_size(axis))
    arrived = lax.all_to_all(pieces, axis, split_axis=0, concat_axis=0, tiled=True)
    return arrived.astype(jnp.float32).sum(axis=0)


def contract_rows(left, right):
    return lax.dot_general(
        left, right, (((0,), (0,)), ((), ())), preferred_element_type=jnp.float32
    )


def contract_last(left, right):
    return lax.dot_general(
        left, right, (((1,), (1,)), ((), ())), preferred_element_type=jnp.float32
    )


def body(hidden_in, down_weight, keep_mask):
    pruned = down_weight * keep_mask.astype(down_weight.dtype)
    all_features = lax.all_gather(hidden_in, "col", axis=1, tiled=True)
    summed = contract_last(all_features, lax.all_gather(pruned, "tok", axis=1, tiled=True))
    layer_cols = summed.astype(jnp.bfloat16)
    scaling = 2.0 / (layer_cols.shape[0] * lax.axis_size("tok"))
    whole = gathered_copies(layer_cols, "col", 1)
    share_rows = whole.shape[0] // lax.axis_size("col")
    layer_out = lax.dynamic_slice_in_dim(whole, lax.axis_index("col") * share_rows, share_rows, 0)
    hessian_term = contract_rows(layer_cols, whole)
    hessian = sent_and_summed((hessian_term * scaling).astype(jnp.bfloat16), "tok", 1)
    return (layer_out, hessian)


def solution(mesh):
    in_specs = (P("tok", "col"), P("col", "tok"), P("col", "tok"))
    out_specs = (P(("tok", "col"), None), P("col", "tok"))
    return jax.shard_map(body, mesh=mesh, in_specs=in_specs, out_specs=out_specs, check_vma=False)
```

profile of v0, /device:TPU:1, one launch (start us, length us, event | category | flops | bytes accessed | tf_op | source)
XLA Modules:
  0.0 347.3 jit_solution(11855072798509974966)
XLA Ops:
  7.2 0.0 all-gather.3.cloned.1.call-start
  7.2 3.4 convert_multiply_fusion
  10.7 0.0 all-gather.3.cloned.1.call-update
  10.7 0.0 all-gather.5.cloned.1.call-start
  10.7 0.7 all-gather.5.cloned.1.call-update
  11.4 65.1 %all-gather.3.cloned.1.call-done = bf16[144,36864]{1,0:T(8,128)(2,1)} async-done(((bf16[144,4608]{1,0:T(8,128)(2,1)}), bf16[144,36864]{1,0:T(8,128)(2,1)}) %all-gather.3.cloned.1.call-update) | async-done | bytes 10616848 | tf_op jit(solution)/shard_map/all_gather | solution.py:48
  76.6 152.6 %all-gather.5.cloned.1.call-done = bf16[256,36864]{1,0:T(8,128)(2,1)} async-done(((bf16[256,1152]{1,0:T(8,128)(2,1)}), bf16[256,36864]{1,0:T(8,128)(2,1)}) %all-gather.5.cloned.1.call-update) | async-done | bytes 18874384 | tf_op jit(solution)/shard_map/all_gather | solution.py:47
  229.1 12.8 %convolution_convert_fusion = bf16[144,256]{1,0:T(8,128)(2,1)S(1)} fusion(bf16[144,36864]{1,0:T(8,128)(2,1)} %all-gather.3.cloned.1.call-done, bf16[256,36864]{1,0:T(8,128)(2,1)} %all-gather.5.cloned.1.call-done), kind=kOutput, calls=%fused_computation.5 | convolution fusion | flops 2717945856 | bytes 29564928 | tf_op jit(solution)/shard_map/dot_general | solution.py:40
  241.9 0.2 broadcast_in_dim.2
  242.1 58.9 %all_to_all.10 = bf16[32,256,144]{1,2,0:T(8,128)(2,1)S(1)} all-to-all(bf16[32,256,144]{1,2,0:T(8,128)(2,1)S(1)} %broadcast_in_dim.2), channel_id=1, replica_groups=mesh['tok'=8,'col'=32] {'col'}, dimensions={0} | all-to-all | bytes 4718592 | tf_op jit(solution)/shard_map/all_to_all | solution.py:15
  300.9 2.0 fusion
  303.0 3.7 %reshape.12 = bf16[144,8,576]{2,1,0:T(8,128)(2,1)} reshape(bf16[144,4608]{1,0:T(8,128)(2,1)} %fusion) | data formatting | bytes 2654208 | tf_op jit(solution)/shard_map/reshape | solution.py:24
  306.7 2.7 copy.10
  309.4 9.1 %all-to-all-start.1 = ((bf16[8,144,576]{2,1,0:T(8,128)(2,1)}), bf16[8,144,576]{2,1,0:T(8,128)(2,1)}, u32[]{:S(2)}, u32[]{:S(2)}) async-start(bf16[8,144,576]{2,1,0:T(8,128)(2,1)} %bitcast.13), calls=%async_computation.1 | async-start | bytes 2949120 | tf_op jit(solution)/shard_map/all_to_all | solution.py:29
  318.4 0.4 constant_dynamic-slice_fusion
  318.8 1.0 copy.8
  319.8 18.3 %all-to-all-done.1 = bf16[8,144,576]{2,1,0:T(8,128)(2,1)} async-done(((bf16[8,144,576]{2,1,0:T(8,128)(2,1)}), bf16[8,144,576]{2,1,0:T(8,128)(2,1)}, u32[]{:S(2)}, u32[]{:S(2)}) %all-to-all-start.1) | async-done | bytes 1327136 | tf_op jit(solution)/shard_map/all_to_all | solution.py:29
  338.1 2.4 convert_reduce_fusion
Async XLA Ops:
  7.2 69.4 %all-gather.3.cloned.1.call-start = ((), (), s32[]{:S(2)}) async-start(), calls=%async_computation.2 | async-start | bytes 11943936 | tf_op jit(solution)/shard_map/all_gather | solution.py:48
  10.7 218.5 %all-gather.5.cloned.1.call-start = ((), (), s32[]{:S(2)}) async-start(), calls=%async_computation.3 | async-start | bytes 19464192 | tf_op jit(solution)/shard_map/all_gather | solution.py:47
  309.4 28.7 %all-to-all-start.1 = ((bf16[8,144,576]{2,1,0:T(8,128)(2,1)}), bf16[8,144,576]{2,1,0:T(8,128)(2,1)}, u32[]{:S(2)}, u32[]{:S(2)}) async-start(bf16[8,144,576]{2,1,0:T(8,128)(2,1)} %bitcast.13), calls=%async_computation.1 | async-start | bytes 2949120 | tf_op jit(solution)/shard_map/all_to_all | solution.py:29
Sparse Core Ops, SparseCore 0:
  10.8 65.7 all-gather.2
  79.3 149.8 all-gather.4
where the time goes:
time: 348 us; the launch traced here: 347 us
  waiting for transfers between devices  237 us (68%)
  blocking collectives  58.9 us (17%)
  matrix products  14.8 us (4%)
  between operations  14.1 us (4%)
  starting transfers between devices  9.16 us (3%)
  local copies, waits for them, and re-layouts  7.93 us (2%)
  other arithmetic  5.8 us (2%)
    all_gather x1, waiting for transfers between devices, body(): all_features = lax.all_gather(hidden_in, 'col', axis=1, tiled=True)  153 us
    all_gather x1, waiting for transfers between devices, body(): lax.all_gather(pruned, 'tok', axis=1, tiled=True)  65.1 us
    all_to_all x1, blocking collectives, from_everyone(): lax.all_to_all(jnp.broadcast_to(x[None], (size, *x.shape)), axis, 0, 0, t...  58.9 us
    all_to_all x1, waiting for transfers between devices, sent_and_summed(): lax.all_to_all(pieces, axis, split_axis=0, concat_axis=0, tiled=True)  18.3 us
    dot_general x1, matrix products, contract_last(): lax.dot_general(left, right, (((1,), (1,)), ((), ())), preferred_element_...  12.8 us
    all_to_all x1, starting transfers between devices, sent_and_summed(): lax.all_to_all(pieces, axis, split_axis=0, concat_axis=0, tiled=True)  9.08 us
  transfers between devices with their start and end apart: 3, of which 3 were waited for; matrix products, arithmetic and copies ran while one was open for 0% of the time, Pallas kernels for 0%

commit v1 on v0

--- a/solution.py
+++ b/solution.py
@@ -2,6 +2,19 @@
 import jax.numpy as jnp
 from jax import lax
 from jax.sharding import PartitionSpec as P
+
+
+def collect(shard, axis, dim):
+    ways = lax.axis_size(axis)
+    up = [(d, (d + 1) % ways) for d in range(ways)]
+    down = [(d, (d - 1) % ways) for d in range(ways)]
+    earlier, later = ([shard], [shard])
+    for _ in range(ways // 2):
+        earlier.append(lax.ppermute(earlier[-1], axis, up))
+    for _ in range((ways - 1) // 2):
+        later.append(lax.ppermute(later[-1], axis, down))
+    line = jnp.concatenate([*earlier[::-1], *later[1:]], axis=dim)
+    return jnp.roll(line, (lax.axis_index(axis) - ways // 2) * shard.shape[dim], axis=dim)
 
 
 def laid_out(pieces, dim):
@@ -45,7 +58,7 @@
 def body(hidden_in, down_weight, keep_mask):
     pruned = down_weight * keep_mask.astype(down_weight.dtype)
     all_features = lax.all_gather(hidden_in, "col", axis=1, tiled=True)
-    summed = contract_last(all_features, lax.all_gather(pruned, "tok", axis=1, tiled=True))
+    summed = contract_last(all_features, collect(pruned, "tok", 1))
     layer_cols = summed.astype(jnp.bfloat16)
     scaling = 2.0 / (layer_cols.shape[0] * lax.axis_size("tok"))
     whole = gathered_copies(layer_cols, "col", 1)

time: 348 us -> 283 us (0.81)
  waiting for transfers between devices: 237 us -> 123 us
  local copies, waits for them, and re-layouts: 7.93 us -> 38.8 us
  starting transfers between devices: 9.16 us -> 28.7 us
    all_gather x1, waiting for transfers between devices: 153 us -> 53.9 us  [body(): all_features = lax.all_gather(hidden_in, 'col', axis=1, tiled=True)]
    all_gather x1 -> x0, waiting for transfers between devices: 65.1 us -> none  [body(): lax.all_gather(pruned, 'tok', axis=1, tiled=True)]
    ppermute x0 -> x7, waiting for transfers between devices: none -> 49.8 us  [the longest x4 48.5 us: collect(): earlier.append(lax.ppermute(earlier[-1], axis, up))]
    unnamed x1 -> x20, local copies, waits for them, and re-layouts: 0.98 us -> 30.7 us
    ppermute x0 -> x7, starting transfers between devices: none -> 19.5 us  [the longest x4 10.1 us: collect(): earlier.append(lax.ppermute(earlier[-1], axis, up))]
  transfers between devices with their start and end apart: 3 -> 9, of which waited for: 3 -> 8; matrix products, arithmetic and copies ran while one was open for 0% -> 12% of each run, Pallas kernels for 0% -> 0%
where the time goes in v1:
time: 283 us; the launch traced here: 282 us
  waiting for transfers between devices  123 us (43%)
  blocking collectives  58.9 us (21%)
  local copies, waits for them, and re-layouts  38.8 us (14%)
  starting transfers between devices  28.7 us (10%)
  matrix products  14.5 us (5%)
  between operations  14.1 us (5%)
  other arithmetic  4.69 us (2%)
    all_to_all x1, blocking collectives, from_everyone(): lax.all_to_all(jnp.broadcast_to(x[None], (size, *x.shape)), axis, 0, 0, t...  58.9 us
    all_gather x1, waiting for transfers between devices, body(): all_features = lax.all_gather(hidden_in, 'col', axis=1, tiled=True)  53.9 us
    ppermute x4, waiting for transfers between devices, collect(): earlier.append(lax.ppermute(earlier[-1], axis, up))  48.5 us
    unnamed x20, local copies, waits for them, and re-layouts  30.7 us
    all_to_all x1, waiting for transfers between devices, sent_and_summed(): lax.all_to_all(pieces, axis, split_axis=0, concat_axis=0, tiled=True)  18.3 us
    dot_general x1, matrix products, contract_last(): lax.dot_general(left, right, (((1,), (1,)), ((), ())), preferred_element_...  12.6 us
    ppermute x4, starting transfers between devices, collect(): earlier.append(lax.ppermute(earlier[-1], axis, up))  10.1 us
    ppermute x3, starting transfers between devices, collect(): later.append(lax.ppermute(later[-1], axis, down))  9.39 us
  transfers between devices with their start and end apart: 9, of which 8 were waited for; matrix products, arithmetic and copies ran while one was open for 12% of the time, Pallas kernels for 0%

profile of v1, /device:TPU:1, one launch (start us, length us, event | category | flops | bytes accessed | tf_op | source)
XLA Modules:
  0.0 282.3 jit_solution(267600912900387181)
XLA Ops:
  10.2 2.6 collective-permute-start
  12.8 14.7 %collective-permute-done = bf16[144,4608]{1,0:T(8,128)(2,1)S(1)} collective-permute-done((bf16[144,4608]{1,0:T(8,128)(2,1)S(1)}, bf16[144,4608]{1,0:T(8,128)(2,1)S(1)}, u32[]{:S(2)}, u32[]{:S(2)}) %collective-permute-start) | collective-permute-done | bytes 1327136 | tf_op jit(solution)/shard_map/ppermute | solution.py:13
  27.6 2.5 collective-permute-start.1
  31.9 12.9 %collective-permute-done.1 = bf16[144,4608]{1,0:T(8,128)(2,1)S(1)} collective-permute-done((bf16[144,4608]{1,0:T(8,128)(2,1)S(1)}, bf16[144,4608]{1,0:T(8,128)(2,1)S(1)}, u32[]{:S(2)}, u32[]{:S(2)}) %collective-permute-start.1) | collective-permute-done | bytes 1327136 | tf_op jit(solution)/shard_map/ppermute | solution.py:13
  44.8 2.5 collective-permute-start.2
  47.7 3.8 %collective-permute-start.5 = (bf16[144,4608]{1,0:T(8,128)(2,1)}, bf16[144,4608]{1,0:T(8,128)(2,1)}, u32[]{:S(2)}, u32[]{:S(2)}) collective-permute-start(bf16[144,4608]{1,0:T(8,128)(2,1)} %collective-permute-done.4), channel_id=1, source_target_pairs={{0,224},{32,0},{64,32},{96,64},{128,96},{160,128},{192,160},{224,1... | collective-permute-start | bytes 3981320 | tf_op jit(solution)/shard_map/ppermute | solution.py:15
  51.4 10.5 %collective-permute-done.2 = bf16[144,4608]{1,0:T(8,128)(2,1)} collective-permute-done((bf16[144,4608]{1,0:T(8,128)(2,1)S(1)}, bf16[144,4608]{1,0:T(8,128)(2,1)}, u32[]{:S(2)}, u32[]{:S(2)}) %collective-permute-start.2) | collective-permute-done | bytes 1327136 | tf_op jit(solution)/shard_map/ppermute | solution.py:13
  62.0 2.6 collective-permute-start.3
  65.5 3.8 %collective-permute-start.6 = (bf16[144,4608]{1,0:T(8,128)(2,1)}, bf16[144,4608]{1,0:T(8,128)(2,1)S(1)}, u32[]{:S(2)}, u32[]{:S(2)}) collective-permute-start(bf16[144,4608]{1,0:T(8,128)(2,1)} %collective-permute-done.5), channel_id=1, source_target_pairs={{0,224},{32,0},{64,32},{96,64},{128,96},{160,128},{192,160},{224,1... | collective-permute-start | bytes 3981320 | tf_op jit(solution)/shard_map/ppermute | solution.py:15
  69.3 10.3 %collective-permute-done.3 = bf16[144,4608]{1,0:T(8,128)(2,1)} collective-permute-done((bf16[144,4608]{1,0:T(8,128)(2,1)}, bf16[144,4608]{1,0:T(8,128)(2,1)}, u32[]{:S(2)}, u32[]{:S(2)}) %collective-permute-start.3) | collective-permute-done | bytes 1327136 | tf_op jit(solution)/shard_map/ppermute | solution.py:13
  82.1 2.5 constant_dynamic-update-slice_fusion.14
  84.6 2.5 constant_dynamic-update-slice_fusion.13
  89.4 2.5 constant_dynamic-update-slice_fusion.10
  91.9 2.5 constant_dynamic-update-slice_fusion.9
  98.1 2.7 constant_dynamic-update-slice_fusion.6
  104.3 2.5 constant_dynamic-update-slice_fusion.2
  106.8 2.5 constant_dynamic-update-slice_fusion.1
  110.5 53.9 %all-gather.2.cloned.1.call-done = bf16[256,36864]{1,0:T(8,128)(2,1)} async-done(((bf16[256,1152]{1,0:T(8,128)(2,1)}), bf16[256,36864]{1,0:T(8,128)(2,1)}) %all-gather.2.cloned.1.call-update) | async-done | bytes 18874384 | tf_op jit(solution)/shard_map/all_gather | solution.py:60
  164.4 12.6 %fusion.3 = bf16[144,256]{1,0:T(8,128)(2,1)S(1)} fusion(bf16[256,36864]{1,0:T(8,128)(2,1)} %all-gather.2.cloned.1.call-done, bf16[144,73728]{1,0:T(8,128)(2,1)} %constant_dynamic-update-slice_fusion, s32[]{:T(128)S(6)} %select_n.17), kind=kOutput, calls=%fused_computation.7 | convolution fusion | flops 2717945856 | bytes 29564932 | tf_op jit(solution)/shard_map/dot_general | solution.py:53
  177.1 58.9 %all_to_all.10 = bf16[32,256,144]{1,2,0:T(8,128)(2,1)S(1)} all-to-all(bf16[32,256,144]{1,2,0:T(8,128)(2,1)S(1)} %broadcast_in_dim.2), channel_id=1, replica_groups=mesh['tok'=8,'col'=32] {'col'}, dimensions={0} | all-to-all | bytes 4718592 | tf_op jit(solution)/shard_map/all_to_all | solution.py:28
  238.0 3.7 %reshape.12 = bf16[144,8,576]{2,1,0:T(8,128)(2,1)} reshape(bf16[144,4608]{1,0:T(8,128)(2,1)} %fusion.2) | data formatting | bytes 2654208 | tf_op jit(solution)/shard_map/reshape | solution.py:37
  241.7 2.7 copy.10
  244.4 9.1 %all-to-all-start.1 = ((bf16[8,144,576]{2,1,0:T(8,128)(2,1)}), bf16[8,144,576]{2,1,0:T(8,128)(2,1)}, u32[]{:S(2)}, u32[]{:S(2)}) async-start(bf16[8,144,576]{2,1,0:T(8,128)(2,1)} %bitcast.12), calls=%async_computation.1 | async-start | bytes 2949120 | tf_op jit(solution)/shard_map/all_to_all | solution.py:42
  254.9 18.3 %all-to-all-done.1 = bf16[8,144,576]{2,1,0:T(8,128)(2,1)} async-done(((bf16[8,144,576]{2,1,0:T(8,128)(2,1)}), bf16[8,144,576]{2,1,0:T(8,128)(2,1)}, u32[]{:S(2)}, u32[]{:S(2)}) %all-to-all-start.1) | async-done | bytes 1327136 | tf_op jit(solution)/shard_map/all_to_all | solution.py:42
  (25 shorter events, 25.2 us)
Async XLA Ops:
  7.2 157.2 %all-gather.2.cloned.1.call-start = ((), (), s32[]{:S(2)}) async-start(), calls=%async_computation.2 | async-start | bytes 19464192 | tf_op jit(solution)/shard_map/all_gather | solution.py:60
  10.2 17.3 %collective-permute-start = (bf16[144,4608]{1,0:T(8,128)(2,1)S(1)}, bf16[144,4608]{1,0:T(8,128)(2,1)S(1)}, u32[]{:S(2)}, u32[]{:S(2)}) collective-permute-start(bf16[144,4608]{1,0:T(8,128)(2,1)S(1)} %convert_multiply_fusion), channel_id=1, source_target_pairs={{0,32},{32,64},{64,96},{96,128},{128,160},{160,192},{192,224},{224... | collective-permute-start | bytes 3981320 | tf_op jit(solution)/shard_map/ppermute | solution.py:13
  27.6 17.2 %collective-permute-start.1 = (bf16[144,4608]{1,0:T(8,128)(2,1)S(1)}, bf16[144,4608]{1,0:T(8,128)(2,1)S(1)}, u32[]{:S(2)}, u32[]{:S(2)}) collective-permute-start(bf16[144,4608]{1,0:T(8,128)(2,1)S(1)} %collective-permute-done), channel_id=1, source_target_pairs={{0,32},{32,64},{64,96},{96,128},{128,160},{160,192},{192,224},{224... | collective-permute-start | bytes 3981320 | tf_op jit(solution)/shard_map/ppermute | solution.py:13
  30.0 17.6 %collective-permute-start.4 = (bf16[144,4608]{1,0:T(8,128)(2,1)S(1)}, bf16[144,4608]{1,0:T(8,128)(2,1)}, u32[]{:S(2)}, u32[]{:S(2)}) collective-permute-start(bf16[144,4608]{1,0:T(8,128)(2,1)S(1)} %convert_multiply_fusion), channel_id=1, source_target_pairs={{0,224},{32,0},{64,32},{96,64},{128,96},{160,128},{192,160},{224,1... | collective-permute-start | bytes 3981320 | tf_op jit(solution)/shard_map/ppermute | solution.py:15
  44.8 2.9 %copy-start = (bf16[144,4608]{1,0:T(8,128)(2,1)}, bf16[144,4608]{1,0:T(8,128)(2,1)S(1)}, u32[]{:S(2)}) copy-start(bf16[144,4608]{1,0:T(8,128)(2,1)S(1)} %collective-permute-done.1) | copy-start | bytes 3981316
  44.8 17.2 %collective-permute-start.2 = (bf16[144,4608]{1,0:T(8,128)(2,1)S(1)}, bf16[144,4608]{1,0:T(8,128)(2,1)}, u32[]{:S(2)}, u32[]{:S(2)}) collective-permute-start(bf16[144,4608]{1,0:T(8,128)(2,1)S(1)} %collective-permute-done.1), channel_id=1, source_target_pairs={{0,32},{32,64},{64,96},{96,128},{128,160},{160,192},{192,224},{224... | collective-permute-start | bytes 3981320 | tf_op jit(solution)/shard_map/ppermute | solution.py:13
  47.7 17.8 %collective-permute-start.5 = (bf16[144,4608]{1,0:T(8,128)(2,1)}, bf16[144,4608]{1,0:T(8,128)(2,1)}, u32[]{:S(2)}, u32[]{:S(2)}) collective-permute-start(bf16[144,4608]{1,0:T(8,128)(2,1)} %collective-permute-done.4), channel_id=1, source_target_pairs={{0,224},{32,0},{64,32},{96,64},{128,96},{160,128},{192,160},{224,1... | collective-permute-start | bytes 3981320 | tf_op jit(solution)/shard_map/ppermute | solution.py:15
  62.0 17.6 %collective-permute-start.3 = (bf16[144,4608]{1,0:T(8,128)(2,1)}, bf16[144,4608]{1,0:T(8,128)(2,1)}, u32[]{:S(2)}, u32[]{:S(2)}) collective-permute-start(bf16[144,4608]{1,0:T(8,128)(2,1)} %collective-permute-done.2), channel_id=1, source_target_pairs={{0,32},{32,64},{64,96},{96,128},{128,160},{160,192},{192,224},{224... | collective-permute-start | bytes 3981320 | tf_op jit(solution)/shard_map/ppermute | solution.py:13
  64.6 36.2 %copy-start.1 = (bf16[144,4608]{1,0:T(8,128)(2,1)S(1)}, bf16[144,4608]{1,0:T(8,128)(2,1)}, u32[]{:S(2)}) copy-start(bf16[144,4608]{1,0:T(8,128)(2,1)} %copy-done) | copy-start | bytes 3981316
  65.5 29.0 %collective-permute-start.6 = (bf16[144,4608]{1,0:T(8,128)(2,1)}, bf16[144,4608]{1,0:T(8,128)(2,1)S(1)}, u32[]{:S(2)}, u32[]{:S(2)}) collective-permute-start(bf16[144,4608]{1,0:T(8,128)(2,1)} %collective-permute-done.5), channel_id=1, source_target_pairs={{0,224},{32,0},{64,32},{96,64},{128,96},{160,128},{192,160},{224,1... | collective-permute-start | bytes 3981320 | tf_op jit(solution)/shard_map/ppermute | solution.py:15
  244.4 28.7 %all-to-all-start.1 = ((bf16[8,144,576]{2,1,0:T(8,128)(2,1)}), bf16[8,144,576]{2,1,0:T(8,128)(2,1)}, u32[]{:S(2)}, u32[]{:S(2)}) async-start(bf16[8,144,576]{2,1,0:T(8,128)(2,1)} %bitcast.12), calls=%async_computation.1 | async-start | bytes 2949120 | tf_op jit(solution)/shard_map/all_to_all | solution.py:42
Sparse Core Ops, SparseCore 0:
  10.7 153.6 all-gather.1
